TPU v7x, 32 devices: a whole 2x2x4 slice. The times are simulated.
32 devices in a mesh: row: 8 (over z, x), col: 4 (over y, core).
Axes of the slice: x: 2, y: 2, z: 4, core: 2. Of those that a mesh axis runs over, the one named last changes fastest.
Arguments:
- prior_scores: float32 [12288, 12288], P('row', 'col'), may hold values from 0.001 to 10
- tiles_first: bfloat16 [96, 5, 128, 128], P('row'), may hold values from 0 to 1, as said below
- columns_first: int32 [96, 5], P('row'), may hold values from 0 to 95, as said below
- tiles_second: bfloat16 [96, 5, 128, 128], P('col'), may hold values from 0 to 1, as said below
- columns_second: int32 [96, 5], P('col'), may hold values from 0 to 95, as said below
Outputs:
- alignment: float32 [12288, 12288], P('row', 'col')
Inputs may be any that keep to these rules, and one draw needn't show every extreme that they name: `tiles_first`: in every block row, the block in the first slot has entries of 0.5 or more on its diagonal. `tiles_second`: in every block row, the block in the first slot has entries of 0.5 or more on its diagonal. `columns_first`: each block row lists 5 different block columns. `columns_second`: each block row lists 5 different block columns.
All inputs are finite; a program needn't handle non-finite values.
Results may differ from a plain program's by a relative error of at most 0.0004.
The roundings to bfloat16 on the way count: a program that leaves them out, or rounds other values in their place, can miss the bound.
Values may be sent and summed in bfloat16 or wider, within the bound.
A program may use at most 192 MiB of HBM per device.

v0:
```python
import jax
import jax.numpy as jnp
from jax import lax
from jax.sharding import PartitionSpec as P

ITERS = 2
mixing = 0.8


def second_product(features, tile_set, columns, inverse):
    tile_size = tile_set.shape[2]
    blocks = features.reshape(-1, tile_size, features.shape[1])
    picked = jnp.take(blocks, columns, axis=0)
    result = jnp.einsum("jsoi,jsin->jon", tile_set, picked, preferred_element_type=jnp.float32)
    result = result.reshape(-1, features.shape[1]) * inverse[:, None]
    return result.astype(jnp.bfloat16)


def first_product(slab_data, tile_set, columns, inverse):
    tile_size = tile_set.shape[2]
    blocks = slab_data.reshape(slab_data.shape[0], -1, tile_size)
    picked = jnp.take(blocks, columns, axis=1)
    result = jnp.einsum("cisk,isok->cio", picked, tile_set, preferred_element_type=jnp.float32)
    result = result.reshape(slab_data.shape[0], -1) * inverse[None, :]
    return result.astype(jnp.bfloat16)


def local(prior_scores, tiles_first, columns_first, tiles_second, columns_second):
    prior_cols = prior_scores.T
    row_count = lax.axis_size("row")
    cell_count = float(
        prior_scores.shape[0] * row_count * prior_scores.shape[1] * lax.axis_size("col")
    )
    all_first, all_columns = (
        lax.all_gather(tiles_first, "row", axis=0, tiled=True),
        lax.all_gather(columns_first, "row", axis=0, tiled=True),
    )
    inverse_first = 1.0 / jnp.sum(all_first, axis=(1, 3), dtype=jnp.float32).reshape(-1)
    inverse_second = 1.0 / jnp.sum(tiles_second, axis=(1, 3), dtype=jnp.float32).reshape(-1)
    prior_sum = lax.psum(jnp.sum(prior_cols), ("row", "col"))
    current_state = prior_cols
    for iteration in range(ITERS):
        current = current_state.astype(jnp.bfloat16)
        gathered = lax.all_gather(current, "col", axis=0, tiled=True)
        mixed_cols = second_product(gathered, tiles_second, columns_second, inverse_second)
        slab_data = lax.all_to_all(mixed_cols, "row", split_axis=0, concat_axis=1, tiled=True)
        propagated = first_product(slab_data, all_first, all_columns, inverse_first)
        partial_value = jnp.sum(propagated.astype(jnp.float32))
        returned = lax.all_to_all(propagated, "row", split_axis=1, concat_axis=0, tiled=True)
        slab_sum = lax.psum(partial_value, ("row", "col"))
        grand_total = mixing * slab_sum + (1.0 - mixing) * prior_sum
        updated = mixing * returned.astype(jnp.float32) + (1.0 - mixing) * prior_cols
        current_state = updated / (grand_total / cell_count)
    return current_state.T


def solution(mesh):
    return jax.shard_map(
        local,
        mesh=mesh,
        in_specs=(
            P("row", "col"),
            P("row", None, None, None),
            P("row", None),
            P("col", None, None, None),
            P("col", None),
        ),
        out_specs=P("row", "col"),
        check_vma=False,
    )
```

profile of v0, /device:TPU:0, one launch (start us, length us, event | category | flops | bytes accessed | tf_op | source)
XLA Modules:
  0.0 1965.2 jit_solution(3482156097374935337)
XLA Ops:
  6.5 20.0 %fusion.28 = (f32[]{:T(128)}, bf16[3072,1536]{0,1:T(8,128)(2,1)}) fusion(f32[1536,3072]{1,0:T(8,128)} %param.9), kind=kLoop, calls=%fused_computation.55 | loop fusion | flops 9437183 | bytes 28311556 | tf_op jit(solution)/shard_map/reduce_sum | solution.py:40
  26.5 0.0 all-gather.5.cloned.1.call-update
  26.6 0.0 all-gather.7.cloned.1.call-start
  26.6 0.7 all-gather.7.cloned.1.call-update
  27.3 0.1 copy.33
  27.5 0.1 copy.37
  27.5 0.1 reshape.154
  27.6 2.7 convert_reduce_fusion.3
  30.4 226.2 %all-gather.5.cloned.1.call-done = bf16[12288,1536]{0,1:T(8,128)(2,1)} async-done(((bf16[3072,1536]{0,1:T(8,128)(2,1)}), bf16[12288,1536]{0,1:T(8,128)(2,1)}) %all-gather.5.cloned.1.call-update) | async-done | bytes 37748752 | tf_op jit(solution)/shard_map/all_gather | solution.py:44
  256.6 48.9 %copy.36 = bf16[12288,1536]{1,0:T(8,128)(2,1)} copy(bf16[12288,1536]{0,1:T(8,128)(2,1)} %all-gather.5.cloned.1.call-done) | data formatting | bytes 75497472 | tf_op jit(solution)/shard_map/all_gather | solution.py:44
  305.6 33.3 %gather_fusion = bf16[120,128,1536]{2,1,0:T(8,128)(2,1)} fusion(bf16[96,128,1536]{2,1,0:T(8,128)(2,1)} %bitcast.87, s32[1024]{0:T(1024)S(1)} %pad_clamp_fusion.1), kind=kCustom, calls=%fused_computation.clone | custom fusion | bytes 94372320 | tf_op jit(solution)/shard_map/jit(_take)/gather | solution.py:13
  338.8 26.4 %fusion.8 = f32[24,1536,128,1]{1,2,3,0:T(8,128)} fusion(bf16[24,5,128,128]{3,2,1,0:T(8,128)(2,1)} %param.12, bf16[24,5,128,1536]{3,2,1,0:T(8,128)(2,1)} %bitcast.93, pred[24,5]{1,0:T(8,128)(4,1)S(1)} %copy.33), kind=kOutput, calls=%fused_computation.12 | convolution fusion | flops 6063390720 | bytes 69992568 | tf_op jit(solution)/shard_map/jsoi,jsin->jon/dot_general | solution.py:14
  365.2 18.7 copy.38
  383.9 11.5 multiply_convert_fusion.3
  395.4 5.4 all-to-all-start
  400.8 292.1 %all-gather = s32[8,12,5]{1,2,0:T(8,128)S(1)} all-gather(s32[1,12,5]{1,2,0:T(8,128)S(1)} %bitcast.99), channel_id=1, replica_groups=mesh['row'=8,'col'=4] {'row'}, dimensions={0}, use_global_device_ids=true | all-gather | bytes 2160 | tf_op jit(solution)/shard_map/all_gather | solution.py:36
  692.9 0.1 reshape.153
  693.0 0.1 copy.32
  693.2 0.1 copy.39
  693.3 0.2 reshape.158
  693.5 0.0 all-gather.7.cloned.1.call-done
  693.5 6.6 convert_reduce_fusion
  700.2 12.6 copy.40
  712.8 23.6 %gather_fusion.1 = bf16[480,384,128]{2,1,0:T(8,128)(2,1)} fusion(bf16[384,96,128]{2,0,1:T(8,128)(2,1)} %copy.40, s32[1024]{0:T(1024)S(1)} %pad_clamp_fusion), kind=kCustom, calls=%fused_computation.1.clone | custom fusion | bytes 94373760 | tf_op jit(solution)/shard_map/jit(_take)/gather | solution.py:22
  736.4 31.3 %convert_reduce_fusion.2 = (f32[]{:T(128)}, f32[96,384,128,1]{1,2,3,0:T(8,128)}) fusion(f32[96,128]{1,0:T(8,128)S(1)} %broadcast_divide_fusion, bf16[96,5,128,128]{3,2,1,0:T(8,128)(2,1)} %all-gather.7.cloned.1.call-done, bf16[96,5,384,128]{3,2,1,0:T(8,128)(2,1)} %bitcast.89, pred[96,5]{1,0:T(8,128)(4,1)S(1)} %copy.32), kind=kOutput, calls=%fused_computation.37 | convolution fusion | flops 6082265088 | bytes 81838560 | tf_op jit(solution)/shard_map/cisk,isok->cio/dot_general | solution.py:23
  767.7 11.8 multiply_convert_fusion.2
  779.5 5.1 all-to-all-start.1
  784.6 0.0 all-gather.9.cloned.1.call-start
  784.6 220.6 %all-reduce = (f32[]{:T(128)}, f32[]{:T(128)}) all-reduce(f32[]{:T(128)} %get-tuple-element.11, f32[]{:T(128)} %get-tuple-element.9), channel_id=1, replica_groups=mesh['row'=8,'col'=4] {'row','col'}, use_global_device_ids=true, to_apply=%region_3.6 | all-reduce | flops 2 | bytes 16 | tf_op jit(solution)/shard_map/psum | solution.py:50
  1006.5 12.4 multiply_bitcast_fusion.1
  1018.9 7.6 copy.52
  1026.5 12.7 fusion.21
  1039.2 227.3 %all-gather.9.cloned.1.call-done = bf16[12288,1536]{0,1:T(8,128)(2,1)} async-done(((bf16[3072,1536]{0,1:T(8,128)(2,1)}), bf16[12288,1536]{0,1:T(8,128)(2,1)}) %all-gather.9.cloned.1.call-update) | async-done | bytes 37748752 | tf_op jit(solution)/shard_map/all_gather | solution.py:44
  1266.6 48.7 %copy.42 = bf16[12288,1536]{1,0:T(8,128)(2,1)} copy(bf16[12288,1536]{0,1:T(8,128)(2,1)} %all-gather.9.cloned.1.call-done) | data formatting | bytes 75497472 | tf_op jit(solution)/shard_map/all_gather | solution.py:44
  1315.2 33.3 %gather_fusion.2 = bf16[120,128,1536]{2,1,0:T(8,128)(2,1)} fusion(bf16[96,128,1536]{2,1,0:T(8,128)(2,1)} %bitcast.86, s32[1024]{0:T(1024)S(1)} %copy-done.5), kind=kCustom, calls=%fused_computation.2.clone | custom fusion | bytes 94372320 | tf_op jit(solution)/shard_map/jit(_take)/gather | solution.py:13
  1348.5 24.3 %fusion.5 = f32[24,1536,128,1]{1,2,3,0:T(8,128)} fusion(bf16[24,5,128,128]{3,2,1,0:T(8,128)(2,1)} %param.12, bf16[24,5,128,1536]{3,2,1,0:T(8,128)(2,1)} %bitcast.92, pred[24,5]{1,0:T(8,128)(4,1)S(1)} %copy-done.15), kind=kOutput, calls=%fused_computation.9 | convolution fusion | flops 6063390720 | bytes 69992568 | tf_op jit(solution)/shard_map/jsoi,jsin->jon/dot_general | solution.py:14
  1372.8 18.7 copy.44
  1391.5 7.6 multiply_convert_fusion.1
  1399.1 212.8 %all_to_all.46 = bf16[8,384,1536]{1,2,0:T(8,128)(2,1)} all-to-all(bf16[8,384,1536]{1,2,0:T(8,128)(2,1)S(1)} %multiply_convert_fusion.1), channel_id=1, replica_groups=mesh['row'=8,'col'=4] {'row'}, dimensions={0} | all-to-all | bytes 18874368 | tf_op jit(solution)/shard_map/all_to_all | solution.py:46
  1611.9 12.6 copy.46
  1624.5 23.7 %gather_fusion.3 = bf16[480,384,128]{2,1,0:T(8,128)(2,1)} fusion(bf16[384,96,128]{2,0,1:T(8,128)(2,1)} %copy.46, s32[1024]{0:T(1024)S(1)} %copy-done.1), kind=kCustom, calls=%fused_computation.3.clone | custom fusion | bytes 94373760 | tf_op jit(solution)/shard_map/jit(_take)/gather | solution.py:22
  1648.2 31.3 %convert_reduce_fusion.1 = (f32[]{:T(128)}, f32[96,384,128,1]{1,2,3,0:T(8,128)}) fusion(f32[96,128]{1,0:T(8,128)S(1)} %copy-done.7, bf16[96,5,128,128]{3,2,1,0:T(8,128)(2,1)} %all-gather.7.cloned.1.call-done, bf16[96,5,384,128]{3,2,1,0:T(8,128)(2,1)} %bitcast.88, pred[96,5]{1,0:T(8,128)(4,1)S(1)} %copy-done.12), kind=kOutput, calls=%fused_computation.33 | convolution fusion | flops 6082265088 | bytes 81838560 | tf_op jit(solution)/shard_map/cisk,isok->cio/dot_general | solution.py:23
  1679.5 11.8 multiply_convert_fusion
  1691.3 5.1 all-to-all-start.3
  1696.4 226.1 %psum.23 = f32[]{:T(128)} all-reduce(f32[]{:T(128)} %get-tuple-element.13), channel_id=1, replica_groups=mesh['row'=8,'col'=4] {'row','col'}, use_global_device_ids=true, to_apply=%region_7.10 | all-reduce | flops 1 | bytes 8 | tf_op jit(solution)/shard_map/psum | solution.py:50
  1923.2 12.4 multiply_bitcast_fusion
  1935.5 7.6 copy.53
  1943.1 15.5 fusion.23
  (48 shorter events, 0.2 us)
Async XLA Ops:
  6.5 20.8 %copy-start.10 = (s32[24,5]{0,1:T(8,128)S(1)}, s32[24,5]{0,1:T(8,128)}, u32[]{:S(2)}) copy-start(s32[24,5]{0,1:T(8,128)} %param.13) | copy-start | bytes 1444
  6.5 250.1 %all-gather.5.cloned.1.call-start = ((), (), s32[]{:S(2)}) async-start(), calls=%async_computation.4 | async-start | bytes 47185920 | tf_op jit(solution)/shard_map/all_gather | solution.py:44
  26.6 666.9 %all-gather.7.cloned.1.call-start = ((), (), s32[]{:S(2)}) async-start(), calls=%async_computation.5 | async-start | bytes 17694720 | tf_op jit(solution)/shard_map/all_gather | solution.py:35
  27.4 311.4 %copy-start.14 = (pred[24,5]{1,0:T(8,128)(4,1)}, pred[24,5]{1,0:T(8,128)(4,1)S(1)}, u32[]{:S(2)}) copy-start(pred[24,5]{1,0:T(8,128)(4,1)S(1)} %copy.33) | copy-start | bytes 364
  30.4 353.5 %copy-start.8 = (f32[8,384]{1,0:T(8,128)}, f32[8,384]{1,0:T(8,128)S(1)}, u32[]{:S(2)}) copy-start(f32[8,384]{1,0:T(8,128)S(1)} %div.47) | copy-start | bytes 36868
  30.4 275.1 %copy-start.4 = (s32[1024]{0:T(1024)}, s32[1024]{0:T(1024)S(1)}, u32[]{:S(2)}) copy-start(s32[1024]{0:T(1024)S(1)} %pad_clamp_fusion.1) | copy-start | bytes 12292
  383.9 16.9 copy-start.13
  395.4 304.7 %all-to-all-start = ((bf16[8,384,1536]{1,2,0:T(8,128)(2,1)}), bf16[8,384,1536]{1,2,0:T(8,128)(2,1)}, u32[]{:S(2)}, u32[]{:S(2)}) async-start(bf16[8,384,1536]{1,2,0:T(8,128)(2,1)} %multiply_convert_fusion.3), calls=%async_computation | async-start | bytes 18874368 | tf_op jit(solution)/shard_map/all_to_all | solution.py:46
  693.1 43.3 %copy-start.11 = (pred[96,5]{1,0:T(8,128)(4,1)}, pred[96,5]{1,0:T(8,128)(4,1)S(1)}, u32[]{:S(2)}) copy-start(pred[96,5]{1,0:T(8,128)(4,1)S(1)} %copy.32) | copy-start | bytes 1444
  693.4 43.0 %copy-start = (s32[1024]{0:T(1024)}, s32[1024]{0:T(1024)S(1)}, u32[]{:S(2)}) copy-start(s32[1024]{0:T(1024)S(1)} %pad_clamp_fusion) | copy-start | bytes 12292
  700.1 36.3 %copy-start.6 = (f32[96,128]{1,0:T(8,128)}, f32[96,128]{1,0:T(8,128)S(1)}, u32[]{:S(2)}) copy-start(f32[96,128]{1,0:T(8,128)S(1)} %broadcast_divide_fusion) | copy-start | bytes 147460
  700.1 67.6 %copy-start.2 = (f32[8,1536]{1,0:T(8,128)}, f32[8,1536]{1,0:T(8,128)S(1)}, u32[]{:S(2)}) copy-start(f32[8,1536]{1,0:T(8,128)S(1)} %div.50) | copy-start | bytes 147460
  779.5 227.0 %all-to-all-start.1 = ((bf16[384,8,1536]{0,2,1:T(8,128)(2,1)}), bf16[384,8,1536]{0,2,1:T(8,128)(2,1)}, u32[]{:S(2)}, u32[]{:S(2)}) async-start(bf16[384,8,1536]{0,2,1:T(8,128)(2,1)} %multiply_convert_fusion.2), calls=%async_computation.1 | async-start | bytes 18874368 | tf_op jit(solution)/shard_map/all_to_all | solution.py:49
  784.6 482.0 %all-gather.9.cloned.1.call-start = ((), (), s32[]{:S(2)}) async-start(), calls=%async_computation.6 | async-start | bytes 47185920 | tf_op jit(solution)/shard_map/all_gather | solution.py:44
  1039.2 276.0 %copy-start.5 = (s32[1024]{0:T(1024)S(1)}, s32[1024]{0:T(1024)}, u32[]{:S(2)}) copy-start(s32[1024]{0:T(1024)} %copy-done.4) | copy-start | bytes 12292
  1315.2 33.3 %copy-start.15 = (pred[24,5]{1,0:T(8,128)(4,1)S(1)}, pred[24,5]{1,0:T(8,128)(4,1)}, u32[]{:S(2)}) copy-start(pred[24,5]{1,0:T(8,128)(4,1)} %copy-done.14) | copy-start | bytes 364
  1372.8 18.7 copy-start.9
  1399.1 225.5 %copy-start.1 = (s32[1024]{0:T(1024)S(1)}, s32[1024]{0:T(1024)}, u32[]{:S(2)}) copy-start(s32[1024]{0:T(1024)} %copy-done) | copy-start | bytes 12292
  1624.5 23.7 %copy-start.7 = (f32[96,128]{1,0:T(8,128)S(1)}, f32[96,128]{1,0:T(8,128)}, u32[]{:S(2)}) copy-start(f32[96,128]{1,0:T(8,128)} %copy-done.6) | copy-start | bytes 147460
  1624.5 23.7 %copy-start.12 = (pred[96,5]{1,0:T(8,128)(4,1)S(1)}, pred[96,5]{1,0:T(8,128)(4,1)}, u32[]{:S(2)}) copy-start(pred[96,5]{1,0:T(8,128)(4,1)} %copy-done.11) | copy-start | bytes 1444
  1648.2 31.3 %copy-start.3 = (f32[8,1536]{1,0:T(8,128)S(1)}, f32[8,1536]{1,0:T(8,128)}, u32[]{:S(2)}) copy-start(f32[8,1536]{1,0:T(8,128)} %copy-done.2) | copy-start | bytes 147460
  1691.3 231.9 %all-to-all-start.3 = ((bf16[384,8,1536]{0,2,1:T(8,128)(2,1)}), bf16[384,8,1536]{0,2,1:T(8,128)(2,1)}, u32[]{:S(2)}, u32[]{:S(2)}) async-start(bf16[384,8,1536]{0,2,1:T(8,128)(2,1)} %multiply_convert_fusion), calls=%async_computation.3 | async-start | bytes 18874368 | tf_op jit(solution)/shard_map/all_to_all | solution.py:49
Sparse Core Ops, SparseCore 0:
  26.7 229.8 all-gather.4
  258.8 288.7 all-gather.6
  1039.4 227.1 all-gather.8
where the time goes:
time: 1970 us
  blocking collectives  952 us (48%)
  waiting for transfers between devices  454 us (23%)
  local copies, waits for them, and re-layouts  290 us (15%)
  other arithmetic  125 us (6%)
  matrix products  113 us (6%)
    all_gather x2, waiting for transfers between devices, local(): gathered = lax.all_gather(current, 'col', axis=0, tiled=True)  454 us
    psum x2, blocking collectives, local(): slab_sum = lax.psum(partial_value, ('row', 'col'))  447 us
    all_gather x1, blocking collectives, local(): lax.all_gather(columns_first, 'row', axis=0, tiled=True)  292 us
    all_to_all x1, blocking collectives, local(): lax.all_to_all(mixed_cols, 'row', split_axis=0, concat_axis=1, tiled=True)  213 us
    all_gather x2, local copies, waits for them, and re-layouts, local(): gathered = lax.all_gather(current, 'col', axis=0, tiled=True)  97.6 us
    gather x2, local copies, waits for them, and re-layouts, second_product(): picked = jnp.take(blocks, columns, axis=0)  66.5 us
    dot_general x2, matrix products, first_product(): jnp.einsum('cisk,isok->cio', picked, tile_set, preferred_element_type=jnp...  62.6 us
    dot_general x2, matrix products, second_product(): jnp.einsum('jsoi,jsin->jon', tile_set, picked, preferred_element_type=jnp...  50.7 us
  transfers between devices with their start and end apart: 6, of which 2 were waited for; matrix products, arithmetic and copies ran while one was open for 8% of the time, Pallas kernels for 0%

commit v1 on v0

--- a/solution.py
+++ b/solution.py
@@ -33,7 +33,9 @@
     )
     all_first, all_columns = (
         lax.all_gather(tiles_first, "row", axis=0, tiled=True),
-        lax.all_gather(columns_first, "row", axis=0, tiled=True),
+        jnp.concatenate(
+            lax.all_to_all(jnp.stack([columns_first] * lax.axis_size("row")), "row", 0, 0), axis=0
+        ),
     )
     inverse_first = 1.0 / jnp.sum(all_first, axis=(1, 3), dtype=jnp.float32).reshape(-1)
     inverse_second = 1.0 / jnp.sum(tiles_second, axis=(1, 3), dtype=jnp.float32).reshape(-1)

time: 1970 us -> 1950 us (0.990)
  blocking collectives: 952 us -> 664 us
  waiting for transfers between devices: 454 us -> 710 us
    all_gather x1 -> x0, blocking collectives: 292 us -> none  [local(): lax.all_gather(columns_first, 'row', axis=0, tiled=True)]
    all_gather x1, waiting for transfers between devices: 0.02 us -> 146 us  [local(): lax.all_gather(tiles_first, 'row', axis=0, tiled=True)]
    all_to_all x1, waiting for transfers between devices: 0.01 us -> 119 us  [local(): lax.all_to_all(mixed_cols, 'row', split_axis=0, concat_axis=1, tiled=True)]
  transfers between devices with their start and end apart: 6 -> 7, of which waited for: 2 -> 4; matrix products, arithmetic and copies ran while one was open for 8% -> 8% of each run, Pallas kernels for 0% -> 0%
where the time goes in v1:
time: 1950 us; the launch traced here: 1940 us
  waiting for transfers between devices  710 us (36%)
  blocking collectives  664 us (34%)
  local copies, waits for them, and re-layouts  291 us (15%)
  other arithmetic  126 us (6%)
  matrix products  113 us (6%)
  starting transfers between devices  22.8 us (1%)
    psum x2, blocking collectives, local(): slab_sum = lax.psum(partial_value, ('row', 'col'))  453 us
    all_gather x2, waiting for transfers between devices, local(): gathered = lax.all_gather(current, 'col', axis=0, tiled=True)  445 us
    all_to_all x1, blocking collectives, local(): lax.all_to_all(mixed_cols, 'row', split_axis=0, concat_axis=1, tiled=True)  212 us
    all_gather x1, waiting for transfers between devices, local(): lax.all_gather(tiles_first, 'row', axis=0, tiled=True)  146 us
    all_to_all x1, waiting for transfers between devices, local(): lax.all_to_all(mixed_cols, 'row', split_axis=0, concat_axis=1, tiled=True)  119 us
    all_gather x2, local copies, waits for them, and re-layouts, local(): gathered = lax.all_gather(current, 'col', axis=0, tiled=True)  97.6 us
    gather x2, local copies, waits for them, and re-layouts, second_product(): picked = jnp.take(blocks, columns, axis=0)  66.4 us
    dot_general x2, matrix products, first_product(): jnp.einsum('cisk,isok->cio', picked, tile_set, preferred_element_type=jnp...  62.4 us
  transfers between devices with their start and end apart: 7, of which 4 were waited for; matrix products, arithmetic and copies ran while one was open for 8% of the time, Pallas kernels for 0%

profile of v1, /device:TPU:0, one launch (start us, length us, event | category | flops | bytes accessed | tf_op | source)
XLA Modules:
  0.0 1942.4 jit_solution(1566009299612423928)
XLA Ops:
  6.5 20.1 %fusion.28 = (f32[]{:T(128)}, bf16[3072,1536]{0,1:T(8,128)(2,1)}) fusion(f32[1536,3072]{1,0:T(8,128)} %param.9), kind=kLoop, calls=%fused_computation.55 | loop fusion | flops 9437183 | bytes 28311556 | tf_op jit(solution)/shard_map/reduce_sum | solution.py:42
  26.7 0.7 all-gather.6.cloned.1.call-update
  27.4 0.6 stack.2
  28.1 7.3 all-to-all-start.1
  35.4 0.1 copy.33
  35.5 0.1 copy.37
  35.6 0.1 reshape.158
  35.7 3.7 convert_reduce_fusion.3
  39.4 217.3 %all-gather.4.cloned.1.call-done = bf16[12288,1536]{0,1:T(8,128)(2,1)} async-done(((bf16[3072,1536]{0,1:T(8,128)(2,1)}), bf16[12288,1536]{0,1:T(8,128)(2,1)}) %all-gather.4.cloned.1.call-update) | async-done | bytes 37748752 | tf_op jit(solution)/shard_map/all_gather | solution.py:46
  256.7 49.0 %copy.36 = bf16[12288,1536]{1,0:T(8,128)(2,1)} copy(bf16[12288,1536]{0,1:T(8,128)(2,1)} %all-gather.4.cloned.1.call-done) | data formatting | bytes 75497472 | tf_op jit(solution)/shard_map/all_gather | solution.py:46
  305.7 33.2 %gather_fusion = bf16[120,128,1536]{2,1,0:T(8,128)(2,1)} fusion(bf16[96,128,1536]{2,1,0:T(8,128)(2,1)} %bitcast.86, s32[1024]{0:T(1024)S(1)} %pad_clamp_fusion.1), kind=kCustom, calls=%fused_computation.clone | custom fusion | bytes 94372320 | tf_op jit(solution)/shard_map/jit(_take)/gather | solution.py:13
  338.9 26.4 %fusion.8 = f32[24,1536,128,1]{1,2,3,0:T(8,128)} fusion(bf16[24,5,128,128]{3,2,1,0:T(8,128)(2,1)} %param.12, bf16[24,5,128,1536]{3,2,1,0:T(8,128)(2,1)} %bitcast.92, pred[24,5]{1,0:T(8,128)(4,1)S(1)} %copy.33), kind=kOutput, calls=%fused_computation.12 | convolution fusion | flops 6063390720 | bytes 69992568 | tf_op jit(solution)/shard_map/jsoi,jsin->jon/dot_general | solution.py:14
  365.2 18.7 copy.38
  383.9 11.5 multiply_convert_fusion.3
  395.4 5.3 all-to-all-start
  400.7 0.1 reshape.112
  400.8 0.1 copy.32
  401.0 0.1 copy.39
  401.1 0.2 reshape.162
  401.3 146.4 %all-gather.6.cloned.1.call-done = bf16[96,5,128,128]{3,2,1,0:T(8,128)(2,1)} async-done(((bf16[12,5,128,128]{3,2,1,0:T(8,128)(2,1)}), bf16[96,5,128,128]{3,2,1,0:T(8,128)(2,1)}) %all-gather.6.cloned.1.call-update) | async-done | bytes 15728656 | tf_op jit(solution)/shard_map/all_gather | solution.py:35
  547.7 6.6 convert_reduce_fusion
  554.3 118.6 %all-to-all-done = bf16[8,384,1536]{1,2,0:T(8,128)(2,1)} async-done(((bf16[8,384,1536]{1,2,0:T(8,128)(2,1)}), bf16[8,384,1536]{1,2,0:T(8,128)(2,1)}, u32[]{:S(2)}, u32[]{:S(2)}) %all-to-all-start) | async-done | bytes 9437216 | tf_op jit(solution)/shard_map/all_to_all | solution.py:48
  672.9 12.6 copy.40
  685.5 23.7 %gather_fusion.1 = bf16[480,384,128]{2,1,0:T(8,128)(2,1)} fusion(bf16[384,96,128]{2,0,1:T(8,128)(2,1)} %copy.40, s32[1024]{0:T(1024)S(1)} %pad_clamp_fusion), kind=kCustom, calls=%fused_computation.1.clone | custom fusion | bytes 94373760 | tf_op jit(solution)/shard_map/jit(_take)/gather | solution.py:22
  709.2 31.2 %convert_reduce_fusion.2 = (f32[]{:T(128)}, f32[96,384,128,1]{1,2,3,0:T(8,128)}) fusion(f32[96,128]{1,0:T(8,128)S(1)} %broadcast_divide_fusion, bf16[96,5,128,128]{3,2,1,0:T(8,128)(2,1)} %all-gather.6.cloned.1.call-done, bf16[96,5,384,128]{3,2,1,0:T(8,128)(2,1)} %bitcast.88, pred[96,5]{1,0:T(8,128)(4,1)S(1)} %copy.32), kind=kOutput, calls=%fused_computation.37 | convolution fusion | flops 6082265088 | bytes 81838560 | tf_op jit(solution)/shard_map/cisk,isok->cio/dot_general | solution.py:23
  740.4 11.8 multiply_convert_fusion.2
  752.2 5.1 all-to-all-start.2
  757.2 0.0 all-gather.8.cloned.1.call-start
  757.3 226.2 %all-reduce = (f32[]{:T(128)}, f32[]{:T(128)}) all-reduce(f32[]{:T(128)} %get-tuple-element.11, f32[]{:T(128)} %get-tuple-element.9), channel_id=1, replica_groups=mesh['row'=8,'col'=4] {'row','col'}, use_global_device_ids=true, to_apply=%region_3.6 | all-reduce | flops 2 | bytes 16 | tf_op jit(solution)/shard_map/psum | solution.py:52
  984.7 12.4 multiply_bitcast_fusion.1
  997.1 7.6 copy.52
  1004.7 12.7 fusion.21
  1017.4 227.3 %all-gather.8.cloned.1.call-done = bf16[12288,1536]{0,1:T(8,128)(2,1)} async-done(((bf16[3072,1536]{0,1:T(8,128)(2,1)}), bf16[12288,1536]{0,1:T(8,128)(2,1)}) %all-gather.8.cloned.1.call-update) | async-done | bytes 37748752 | tf_op jit(solution)/shard_map/all_gather | solution.py:46
  1244.7 48.7 %copy.42 = bf16[12288,1536]{1,0:T(8,128)(2,1)} copy(bf16[12288,1536]{0,1:T(8,128)(2,1)} %all-gather.8.cloned.1.call-done) | data formatting | bytes 75497472 | tf_op jit(solution)/shard_map/all_gather | solution.py:46
  1293.4 33.2 %gather_fusion.2 = bf16[120,128,1536]{2,1,0:T(8,128)(2,1)} fusion(bf16[96,128,1536]{2,1,0:T(8,128)(2,1)} %bitcast.85, s32[1024]{0:T(1024)S(1)} %copy-done.5), kind=kCustom, calls=%fused_computation.2.clone | custom fusion | bytes 94372320 | tf_op jit(solution)/shard_map/jit(_take)/gather | solution.py:13
  1326.5 24.4 %fusion.5 = f32[24,1536,128,1]{1,2,3,0:T(8,128)} fusion(bf16[24,5,128,128]{3,2,1,0:T(8,128)(2,1)} %param.12, bf16[24,5,128,1536]{3,2,1,0:T(8,128)(2,1)} %bitcast.91, pred[24,5]{1,0:T(8,128)(4,1)S(1)} %copy-done.15), kind=kOutput, calls=%fused_computation.9 | convolution fusion | flops 6063390720 | bytes 69992568 | tf_op jit(solution)/shard_map/jsoi,jsin->jon/dot_general | solution.py:14
  1350.9 18.6 copy.44
  1369.6 7.6 multiply_convert_fusion.1
  1377.2 211.8 %all_to_all.51 = bf16[8,384,1536]{1,2,0:T(8,128)(2,1)} all-to-all(bf16[8,384,1536]{1,2,0:T(8,128)(2,1)S(1)} %multiply_convert_fusion.1), channel_id=1, replica_groups=mesh['row'=8,'col'=4] {'row'}, dimensions={0} | all-to-all | bytes 18874368 | tf_op jit(solution)/shard_map/all_to_all | solution.py:48
  1589.0 12.6 copy.46
  1601.6 23.7 %gather_fusion.3 = bf16[480,384,128]{2,1,0:T(8,128)(2,1)} fusion(bf16[384,96,128]{2,0,1:T(8,128)(2,1)} %copy.46, s32[1024]{0:T(1024)S(1)} %copy-done.1), kind=kCustom, calls=%fused_computation.3.clone | custom fusion | bytes 94373760 | tf_op jit(solution)/shard_map/jit(_take)/gather | solution.py:22
  1625.3 31.2 %convert_reduce_fusion.1 = (f32[]{:T(128)}, f32[96,384,128,1]{1,2,3,0:T(8,128)}) fusion(f32[96,128]{1,0:T(8,128)S(1)} %copy-done.7, bf16[96,5,128,128]{3,2,1,0:T(8,128)(2,1)} %all-gather.6.cloned.1.call-done, bf16[96,5,384,128]{3,2,1,0:T(8,128)(2,1)} %bitcast.87, pred[96,5]{1,0:T(8,128)(4,1)S(1)} %copy-done.12), kind=kOutput, calls=%fused_computation.33 | convolution fusion | flops 6082265088 | bytes 81838560 | tf_op jit(solution)/shard_map/cisk,isok->cio/dot_general | solution.py:23
  1656.5 11.8 multiply_convert_fusion
  1668.3 5.1 all-to-all-start.4
  1673.4 226.3 %psum.23 = f32[]{:T(128)} all-reduce(f32[]{:T(128)} %get-tuple-element.13), channel_id=1, replica_groups=mesh['row'=8,'col'=4] {'row','col'}, use_global_device_ids=true, to_apply=%region_7.10 | all-reduce | flops 1 | bytes 8 | tf_op jit(solution)/shard_map/psum | solution.py:52
  1900.4 12.4 multiply_bitcast_fusion
  1912.7 7.6 copy.53
  1920.3 15.5 fusion.23
  (50 shorter events, 0.2 us)
Async XLA Ops:
  6.5 20.9 %copy-start.13 = (s32[12,5]{0,1:T(8,128)S(1)}, s32[12,5]{0,1:T(8,128)}, u32[]{:S(2)}) copy-start(s32[12,5]{0,1:T(8,128)} %param.11) | copy-start | bytes 724
  6.5 28.8 %copy-start.10 = (s32[24,5]{0,1:T(8,128)S(1)}, s32[24,5]{0,1:T(8,128)}, u32[]{:S(2)}) copy-start(s32[24,5]{0,1:T(8,128)} %param.13) | copy-start | bytes 1444
  6.5 250.2 %all-gather.4.cloned.1.call-start = ((), (), s32[]{:S(2)}) async-start(), calls=%async_computation.5 | async-start | bytes 47185920 | tf_op jit(solution)/shard_map/all_gather | solution.py:46
  26.7 521.0 %all-gather.6.cloned.1.call-start = ((), (), s32[]{:S(2)}) async-start(), calls=%async_computation.6 | async-start | bytes 17694720 | tf_op jit(solution)/shard_map/all_gather | solution.py:35
  28.1 367.4 %all-to-all-start.1 = ((s32[8,12,5]{1,2,0:T(8,128)}), s32[8,12,5]{1,2,0:T(8,128)S(1)}, u32[]{:S(2)}, u32[]{:S(2)}) async-start(s32[8,12,5]{1,2,0:T(8,128)} %stack.2), calls=%async_computation.1 | async-start | bytes 65536 | tf_op jit(solution)/shard_map/all_to_all | solution.py:37
  35.5 303.4 %copy-start.14 = (pred[24,5]{1,0:T(8,128)(4,1)}, pred[24,5]{1,0:T(8,128)(4,1)S(1)}, u32[]{:S(2)}) copy-start(pred[24,5]{1,0:T(8,128)(4,1)S(1)} %copy.33) | copy-start | bytes 364
  39.4 344.5 %copy-start.8 = (f32[8,384]{1,0:T(8,128)}, f32[8,384]{1,0:T(8,128)S(1)}, u32[]{:S(2)}) copy-start(f32[8,384]{1,0:T(8,128)S(1)} %div.47) | copy-start | bytes 36868
  39.4 266.3 %copy-start.4 = (s32[1024]{0:T(1024)}, s32[1024]{0:T(1024)S(1)}, u32[]{:S(2)}) copy-start(s32[1024]{0:T(1024)S(1)} %pad_clamp_fusion.1) | copy-start | bytes 12292
  395.4 277.5 %all-to-all-start = ((bf16[8,384,1536]{1,2,0:T(8,128)(2,1)}), bf16[8,384,1536]{1,2,0:T(8,128)(2,1)}, u32[]{:S(2)}, u32[]{:S(2)}) async-start(bf16[8,384,1536]{1,2,0:T(8,128)(2,1)} %multiply_convert_fusion.3), calls=%async_computation | async-start | bytes 18874368 | tf_op jit(solution)/shard_map/all_to_all | solution.py:48
  400.9 308.2 %copy-start.11 = (pred[96,5]{1,0:T(8,128)(4,1)}, pred[96,5]{1,0:T(8,128)(4,1)S(1)}, u32[]{:S(2)}) copy-start(pred[96,5]{1,0:T(8,128)(4,1)S(1)} %copy.32) | copy-start | bytes 1444
  401.2 307.9 %copy-start = (s32[1024]{0:T(1024)}, s32[1024]{0:T(1024)S(1)}, u32[]{:S(2)}) copy-start(s32[1024]{0:T(1024)S(1)} %pad_clamp_fusion) | copy-start | bytes 12292
  554.3 154.9 %copy-start.6 = (f32[96,128]{1,0:T(8,128)}, f32[96,128]{1,0:T(8,128)S(1)}, u32[]{:S(2)}) copy-start(f32[96,128]{1,0:T(8,128)S(1)} %broadcast_divide_fusion) | copy-start | bytes 147460
  554.3 186.1 %copy-start.2 = (f32[8,1536]{1,0:T(8,128)}, f32[8,1536]{1,0:T(8,128)S(1)}, u32[]{:S(2)}) copy-start(f32[8,1536]{1,0:T(8,128)S(1)} %div.50) | copy-start | bytes 147460
  752.2 232.6 %all-to-all-start.2 = ((bf16[384,8,1536]{0,2,1:T(8,128)(2,1)}), bf16[384,8,1536]{0,2,1:T(8,128)(2,1)}, u32[]{:S(2)}, u32[]{:S(2)}) async-start(bf16[384,8,1536]{0,2,1:T(8,128)(2,1)} %multiply_convert_fusion.2), calls=%async_computation.2 | async-start | bytes 18874368 | tf_op jit(solution)/shard_map/all_to_all | solution.py:51
  757.2 487.5 %all-gather.8.cloned.1.call-start = ((), (), s32[]{:S(2)}) async-start(), calls=%async_computation.7 | async-start | bytes 47185920 | tf_op jit(solution)/shard_map/all_gather | solution.py:46
  1017.4 275.9 %copy-start.5 = (s32[1024]{0:T(1024)S(1)}, s32[1024]{0:T(1024)}, u32[]{:S(2)}) copy-start(s32[1024]{0:T(1024)} %copy-done.4) | copy-start | bytes 12292
  1293.4 33.2 %copy-start.15 = (pred[24,5]{1,0:T(8,128)(4,1)S(1)}, pred[24,5]{1,0:T(8,128)(4,1)}, u32[]{:S(2)}) copy-start(pred[24,5]{1,0:T(8,128)(4,1)} %copy-done.14) | copy-start | bytes 364
  1350.9 18.6 copy-start.9
  1377.2 224.4 %copy-start.1 = (s32[1024]{0:T(1024)S(1)}, s32[1024]{0:T(1024)}, u32[]{:S(2)}) copy-start(s32[1024]{0:T(1024)} %copy-done) | copy-start | bytes 12292
  1601.6 23.7 %copy-start.7 = (f32[96,128]{1,0:T(8,128)S(1)}, f32[96,128]{1,0:T(8,128)}, u32[]{:S(2)}) copy-start(f32[96,128]{1,0:T(8,128)} %copy-done.6) | copy-start | bytes 147460
  1601.6 23.7 %copy-start.12 = (pred[96,5]{1,0:T(8,128)(4,1)S(1)}, pred[96,5]{1,0:T(8,128)(4,1)}, u32[]{:S(2)}) copy-start(pred[96,5]{1,0:T(8,128)(4,1)} %copy-done.11) | copy-start | bytes 1444
  1625.3 31.2 %copy-start.3 = (f32[8,1536]{1,0:T(8,128)S(1)}, f32[8,1536]{1,0:T(8,128)}, u32[]{:S(2)}) copy-start(f32[8,1536]{1,0:T(8,128)} %copy-done.2) | copy-start | bytes 147460
  1668.3 232.0 %all-to-all-start.4 = ((bf16[384,8,1536]{0,2,1:T(8,128)(2,1)}), bf16[384,8,1536]{0,2,1:T(8,128)(2,1)}, u32[]{:S(2)}, u32[]{:S(2)}) async-start(bf16[384,8,1536]{0,2,1:T(8,128)(2,1)} %multiply_convert_fusion), calls=%async_computation.4 | async-start | bytes 18874368 | tf_op jit(solution)/shard_map/all_to_all | solution.py:51
Sparse Core Ops, SparseCore 0:
  26.8 229.8 all-gather.3
  258.9 288.7 all-gather.5
  1017.5 227.1 all-gather.7
